TPU v7x, 256 devices: a whole 4x4x8 slice. The times are simulated.
256 devices in a mesh: seq: 32 (over z, y_hi, core), batch: 8 (over x, y_lo).
Axes of the slice: x: 4, y: 4 (y_hi: 2, y_lo: 2; y = y_hi * 2 + y_lo), z: 8, core: 2. Of those that a mesh axis runs over, the one named last changes fastest.
Arguments:
- queries: bfloat16 [32768, 1792], P(('batch', 'seq')), parts along dimension 0, may hold values from -128 to 128
- keys: bfloat16 [32768, 256], P(('batch', 'seq')), parts along dimension 0, may hold values from -4 to 4
- values: bfloat16 [32768, 256], P(('batch', 'seq')), parts along dimension 0, may hold values from -4 to 4
- out_grad: bfloat16 [32768, 1792], P(('batch', 'seq')), parts along dimension 0, may hold values from -24 to 24
- row_delta: float32 [32768, 14], P(('batch', 'seq')), parts along dimension 0, may hold values from -6 to 6
- layer_input: bfloat16 [32768, 3584], P(('batch', 'seq')), parts along dimension 0, may hold values from -6 to 6
- norm_gain: float32 [3584], replicated, may hold values from 0.25 to 1.75
- qkv_weight: bfloat16 [3584, 2304], P('seq'), may hold values from -0.5 to 0.5
- block_order: int32 [512], P('batch'), parts along dimension 0, may hold values from 0 to 63, as said below
- block_mask: int32 [512, 64], P('batch'), parts along dimension 0, may hold values from 0 to 1, as said below
- frame_owner: int32 [256], P('batch'), parts along dimension 0, may hold values from 0 to 31, as said below
- vision_features: bfloat16 [256, 128, 1152], P(('batch', 'seq')), parts along dimension 0, may hold values from -6 to 6
- post_gain: float32 [1152], replicated, may hold values from 0.25 to 1.75
- projector: bfloat16 [1152, 3584], replicated, may hold values from -0.1875 to 0.1875
Outputs:
- token_grad: bfloat16 [32768, 3584], P(('batch', 'seq')), parts along dimension 0
- encoder_grad: bfloat16 [256, 128, 1152], P(('batch', 'seq')), parts along dimension 0
There are 8 independent parts, one for each index of `batch`. A program takes and returns all parts, laid end to end along the dimension named above; an argument that names none is the same for every part. Nothing has to cross between parts.
Inputs may be any that keep to these rules, and one draw needn't show every extreme that they name: `block_order`: entries 2i and 2i + 1 are the blocks of device i of seq; all entries together are a permutation; each device's two blocks sum to 63; for every frame f, blocks 2f and 2f + 1 lie on devices 2j and 2j + 1 for some j. `block_mask`: 1 on the diagonal, 0 above it. `frame_owner`: every device of seq owns exactly one frame, and the owner of frame f holds block 2f or block 2f + 1.
All inputs are finite; a program needn't handle non-finite values.
Results may differ from a plain program's by a relative error of at most 0.012.
Values may be sent and summed in bfloat16 or wider, within the bound.
A program may use at most 128 MiB of HBM per device.

v0:
```python
import jax
import jax.numpy as jnp
from jax import lax
from jax.sharding import PartitionSpec as P

HQ = 14
KVH = 2
HD = 128


EPSILON = 1e-06
NEGATIVE = -1e30


def shifted(value, axis, steps):
    count = lax.axis_size(axis)
    pairs = [(source, (source + steps) % count) for source in range(count)]
    return lax.ppermute(value, axis, pairs)


def for_sending(array):
    return jax.tree.map(lambda a: a.astype(jnp.bfloat16) if a.dtype == jnp.float32 else a, array)


def swapped(array, axis, apart):
    return lax.ppermute(array, axis, [(i, i ^ 1 << apart) for i in range(lax.axis_size(axis))])


def pick_blocks(block_order, slot_ids):
    table = jnp.arange(block_order.shape[0], dtype=jnp.int32)
    matched = slot_ids[:, None] == table[None, :]
    return jnp.sum(jnp.where(matched, block_order[None, :], 0), axis=1)


def key_mask(query_pos, query_live, block_order, first_row, key_rows, half_len):
    row_ids = first_row + jnp.arange(key_rows, dtype=jnp.int32)
    key_blocks = pick_blocks(block_order, row_ids // half_len)
    key_pos = key_blocks * half_len + row_ids % half_len
    table = jnp.arange(block_order.shape[0], dtype=jnp.int32)
    key_onehot = (key_blocks[:, None] == table[None, :]).astype(jnp.int32)
    allowed = jnp.dot(query_live, key_onehot.T)
    return (allowed > 0) & (key_pos[None, :] <= query_pos[:, None])


def score_block(query_part, keys_here, scaling):
    return (
        jnp.einsum("qkgd,tkd->kgqt", query_part, keys_here, preferred_element_type=jnp.float32)
        * scaling
    )


def block_grads(
    query_part, grad_part, lse_part, delta_part, keys_here, values_here, allowed, scaling
):
    score = score_block(query_part, keys_here, scaling)
    prob = jnp.where(allowed, jnp.exp(score - lse_part[..., None]), 0.0)
    prob_low = prob.astype(jnp.bfloat16)
    value_add = jnp.einsum(
        "kgqt,qkgd->tkd", prob_low, grad_part, preferred_element_type=jnp.float32
    )
    prob_grad = jnp.einsum(
        "qkgd,tkd->kgqt", grad_part, values_here, preferred_element_type=jnp.float32
    )
    score_grad = (prob * (prob_grad - delta_part[..., None])).astype(jnp.bfloat16)
    query_add = jnp.einsum(
        "kgqt,tkd->qkgd", score_grad, keys_here, preferred_element_type=jnp.float32
    )
    key_add = jnp.einsum(
        "kgqt,qkgd->tkd", score_grad, query_part, preferred_element_type=jnp.float32
    )
    return (query_add, key_add, value_add)


def body(
    queries,
    keys,
    values,
    out_grad,
    row_delta,
    layer_input,
    norm_gain,
    qkv_weight,
    block_order,
    block_mask,
    frame_owner,
    vision_features,
    post_gain,
    projector,
):
    tok_rows = queries.shape[0]
    half_len = tok_rows // 2
    cycle_size = lax.axis_size("seq")
    my_index = lax.axis_index("seq")
    group_size = HQ // KVH
    scaling = HD ** (-0.5)
    block_count = block_order.shape[0]
    block_table = jnp.arange(block_count, dtype=jnp.int32)
    my_blocks = lax.dynamic_slice_in_dim(block_order, 2 * my_index, 2, 0)
    query_pos = (
        my_blocks[:, None] * half_len + jnp.arange(half_len, dtype=jnp.int32)[None, :]
    ).reshape(tok_rows)
    my_onehot = (my_blocks[:, None] == block_table[None, :]).astype(jnp.int32)
    query_live = jnp.repeat(jnp.dot(my_onehot, block_mask), half_len, axis=0)
    query_five = queries.reshape(tok_rows, KVH, group_size, HD)
    grad_five = out_grad.reshape(tok_rows, KVH, group_size, HD)
    key_three = keys.reshape(tok_rows, KVH, HD)
    value_three = values.reshape(tok_rows, KVH, HD)
    delta_rows = jnp.transpose(row_delta.reshape(tok_rows, KVH, group_size), (1, 2, 0))
    zero_stats = (
        jnp.full((KVH, group_size, tok_rows), NEGATIVE, jnp.float32),
        jnp.zeros((KVH, group_size, tok_rows), jnp.float32),
    )
    key_piece = lax.all_gather(keys, "seq", axis=0, tiled=True)
    shards = key_piece.shape[0] // tok_rows
    stacked = key_piece.reshape(shards, tok_rows, KVH, HD)

    def absorb(current, shard_entry):
        top_now, total_now = current
        keys_here, shard_index = shard_entry
        allowed = key_mask(
            query_pos, query_live, block_order, shard_index * tok_rows, tok_rows, half_len
        )
        score = score_block(query_five, keys_here, scaling)
        top_next = jnp.maximum(top_now, jnp.max(jnp.where(allowed, score, NEGATIVE), axis=-1))
        spread = jnp.where(allowed, jnp.exp(score - top_next[..., None]), 0.0)
        return (
            (top_next, total_now * jnp.exp(top_now - top_next) + jnp.sum(spread, axis=-1)),
            None,
        )

    result, unused = lax.scan(absorb, zero_stats, (stacked, jnp.arange(shards, dtype=jnp.int32)))
    lse_rows = result[0] + jnp.log(result[1])

    def absorb_source(kv_pair, kv_grads, source):
        allowed = key_mask(
            query_pos, query_live, block_order, source * tok_rows, tok_rows, half_len
        )
        query_add, key_add, value_add = block_grads(
            query_five, grad_five, lse_rows, delta_rows, kv_pair[0], kv_pair[1], allowed, scaling
        )
        return (query_add, (kv_grads[0] + key_add, kv_grads[1] + value_add))

    query_acc = jnp.zeros((tok_rows, KVH, group_size, HD), jnp.float32)

    def pass_grads(kv_grads):
        return shifted(kv_grads, "seq", 1)

    def cycle_turn(step_index, running):
        kv_pair, kv_grads, query_sum = running
        source = (my_index - step_index) % cycle_size
        query_add, kv_grads = absorb_source(kv_pair, kv_grads, source)
        kv_pair = jax.tree.map(
            lambda part, own: part.astype(own.dtype),
            shifted(for_sending(kv_pair), "seq", 1),
            kv_pair,
        )
        return (kv_pair, pass_grads(kv_grads), query_sum + query_add)

    zero_grads = (
        jnp.zeros((tok_rows, KVH, HD), jnp.float32),
        jnp.zeros((tok_rows, KVH, HD), jnp.float32),
    )
    kv_pair, kv_grads, query_acc = lax.fori_loop(
        0, cycle_size - 1, cycle_turn, ((key_three, value_three), zero_grads, query_acc)
    )
    query_add, kv_grads = absorb_source(kv_pair, kv_grads, (my_index + 1) % cycle_size)
    key_sum, value_sum = pass_grads(kv_grads)
    query_acc = query_acc + query_add
    query_grad = (query_acc * scaling).astype(jnp.bfloat16).reshape(tok_rows, HQ * HD)
    key_grad = (key_sum * scaling).astype(jnp.bfloat16).reshape(tok_rows, KVH * HD)
    value_grad = value_sum.astype(jnp.bfloat16).reshape(tok_rows, KVH * HD)
    head_grads = jnp.concatenate([query_grad, key_grad, value_grad], axis=1)
    norm_grad = jnp.dot(
        head_grads,
        lax.all_gather(qkv_weight, "seq", axis=0, tiled=True).T,
        preferred_element_type=jnp.float32,
    ).astype(jnp.bfloat16)
    inputs = layer_input.astype(jnp.float32)
    inverse = lax.rsqrt(jnp.mean(inputs * inputs, axis=1, keepdims=True) + EPSILON)
    scaled = norm_grad.astype(jnp.float32) * norm_gain
    token_grad = (
        inverse * scaled - inputs * inverse**3 * jnp.mean(scaled * inputs, axis=1, keepdims=True)
    ).astype(jnp.bfloat16)
    frame_table = jnp.arange(frame_owner.shape[0], dtype=jnp.int32)
    my_frame = jnp.sum(jnp.where(frame_owner == my_index, frame_table, 0))
    keep_first = my_blocks[0] // 2 == my_frame
    kept_block = jnp.where(keep_first, my_blocks[0], my_blocks[1])
    leading = kept_block % 2 == 0
    halves = token_grad.reshape(2, half_len, token_grad.shape[1])
    kept = jnp.where(keep_first, halves[0], halves[1])
    sending = jnp.where(keep_first, halves[1], halves[0])
    received = swapped(sending, "seq", 0)
    frame_rows = jnp.where(
        leading,
        jnp.concatenate([kept, received], axis=0),
        jnp.concatenate([received, kept], axis=0),
    )
    post_grad = jnp.dot(frame_rows, projector.T, preferred_element_type=jnp.float32)
    features = vision_features[0].astype(jnp.float32)
    centered = features - jnp.mean(features, axis=1, keepdims=True)
    deviation = lax.rsqrt(jnp.mean(centered * centered, axis=1, keepdims=True) + EPSILON)
    normed = centered * deviation
    weighted = post_grad * post_gain
    encoder_grad = (
        deviation
        * (
            weighted
            - jnp.mean(weighted, axis=1, keepdims=True)
            - normed * jnp.mean(weighted * normed, axis=1, keepdims=True)
        )
    ).astype(jnp.bfloat16)
    return (token_grad, encoder_grad[None])


def solution(mesh):
    placed = (
        P(("batch", "seq"), None),
        P(("batch", "seq"), None),
        P(("batch", "seq"), None),
        P(("batch", "seq"), None),
        P(("batch", "seq"), None),
        P(("batch", "seq"), None),
        P(),
        P("seq", None),
        P("batch"),
        P("batch", None),
        P("batch"),
        P(("batch", "seq"), None, None),
        P(),
        P(),
    )
    return jax.shard_map(
        body,
        mesh=mesh,
        in_specs=placed,
        out_specs=(P(("batch", "seq"), None), P(("batch", "seq"), None, None)),
        check_vma=False,
    )
```

profile of v0, /device:TPU:1, one launch (start us, length us, event | category | flops | bytes accessed | tf_op | source)
XLA Modules:
  0.0 636.3 jit_solution(7462449459570991946)
XLA Ops:
  19.7 75.1 %all-gather.3.cloned.1.call-done = bf16[4096,256]{1,0:T(8,128)(2,1)} async-done(((bf16[128,256]{1,0:T(8,128)(2,1)}), bf16[4096,256]{1,0:T(8,128)(2,1)}) %all-gather.3.cloned.1.call-update) | async-done | bytes 2097168 | tf_op jit(solution)/shard_map/all_gather | solution.py:113
  94.9 4.0 reshape.248
  98.9 104.3 %while.40 = (s32[]{:T(128)}, f32[2,7,128]{2,1,0:T(8,128)S(1)}, f32[2,7,128]{2,1,0:T(8,128)S(1)}, s32[32]{0:T(128)S(1)}, s32[64]{0:T(128)S(1)}, /*index=5*/bf16[3...) while((s32[]{:T(128)}, f32[2,7,128]{2,1,0:T(8,128)S(1)}, ...), condition=%wide.region_5.6_spmd.clone, body=%wide.region_1.5_spmd.clone.sunk | while | flops 62288384 | bytes 2704812 | solution.py:131
  203.3 390.5 %while.41 = (s32[]{:T(128)}, bf16[128,2,128]{2,0,1:T(8,128)(2,1)S(1)}, bf16[128,2,128]{2,0,1:T(8,128)(2,1)}, f32[128,2,128]{2,0,1:T(8,128)S(1)}, f32[128,2,128]{...) while((s32[]{:T(128)}, ...), condition=%wide.region_8.9_spmd.clone, body=%wide.region_6.8_spmd.clone.sunk | while | flops 297914112 | bytes 10474220 | solution.py:163
  212.8 4.0 collective-permute-start
  217.7 3.2 collective-permute-start.1
  222.4 5.0 collective-permute-start.2
  230.7 4.0 collective-permute-start
  237.0 3.4 collective-permute-start.2
  243.7 4.0 collective-permute-start
  255.8 4.0 collective-permute-start
  268.3 4.0 collective-permute-start
  281.1 4.0 collective-permute-start
  293.3 4.0 collective-permute-start
  299.6 3.4 collective-permute-start.2
  306.4 4.0 collective-permute-start
  312.7 3.6 collective-permute-start.2
  319.6 4.0 collective-permute-start
  331.4 4.0 collective-permute-start
  337.7 4.9 collective-permute-start.2
  345.9 4.0 collective-permute-start
  357.7 4.0 collective-permute-start
  369.9 4.0 collective-permute-start
  381.7 4.0 collective-permute-start
  394.1 4.0 collective-permute-start
  406.4 4.0 collective-permute-start
  412.7 3.4 collective-permute-start.2
  419.5 4.0 collective-permute-start
  431.3 4.0 collective-permute-start
  443.4 4.0 collective-permute-start
  455.5 4.0 collective-permute-start
  467.9 4.0 collective-permute-start
  480.8 4.0 collective-permute-start
  493.0 4.0 collective-permute-start
  499.3 3.4 collective-permute-start.2
  506.1 4.0 collective-permute-start
  512.4 3.6 collective-permute-start.2
  519.3 4.0 collective-permute-start
  531.1 4.0 collective-permute-start
  537.4 4.9 collective-permute-start.2
  545.6 4.0 collective-permute-start
  557.4 4.0 collective-permute-start
  569.6 4.0 collective-permute-start
  581.4 4.0 collective-permute-start
  596.8 4.1 collective-permute-start.4
  603.8 9.2 %fusion.34 = (f32[128]{0:T(128)S(1)}, f32[128]{0:T(128)S(1)}, f32[128,3584]{1,0:T(8,128)S(1)}) fusion(bf16[128,3584]{1,0:T(8,128)(2,1)S(1)} %copy-done.5, f32[3584]{0:T(1024)S(1)} %copy-done.10, bf16[3584,2304]{1,0:T(8,128)(2,1)} %all-gather.5.cloned.1.call-done, bf16[128,256]{0,1:T(8,128)(2,1)S(1)} %bitcast.234, bf16[128,256]{0,1:T(8,128)(2,1)S(1)} %bitcast.235, ...), kind=kOutput, calls=%fused_computation.69 | convolution fusion | flops 2119368448 | bytes 19872768 | tf_op jit(solution)/shard_map/dot_general | solution.py:173
  614.8 6.1 collective-permute-start.6
  622.4 6.1 fusion.87
  (1176 shorter events, 329.4 us)
Async XLA Ops:
  7.2 87.7 %all-gather.3.cloned.1.call-start = ((), (), s32[]{:S(2)}) async-start(), calls=%async_computation | async-start | bytes 2162688 | tf_op jit(solution)/shard_map/all_gather | solution.py:113
  7.9 595.9 %all-gather.5.cloned.1.call-start = ((), (), s32[]{:S(2)}) async-start(), calls=%async_computation.1 | async-start | bytes 17031168 | tf_op jit(solution)/shard_map/all_gather | solution.py:175
  203.3 7.2 %collective-permute-start = (bf16[128,2,128]{2,0,1:T(8,128)(2,1)S(1)}, bf16[128,2,128]{2,0,1:T(8,128)(2,1)S(1)}, u32[]{:S(2)}, u32[]{:S(2)}) collective-permute-start(bf16[128,2,128]{2,0,1:T(8,128)(2,1)S(1)} %copy.108), channel_id=1, source_target_pairs={{0,8},{8,16},{16,24},{24,32},{32,40},{40,48},{48,56},{56,64},{64,7... | collective-permute-start | bytes 196616 | tf_op jit(solution)/shard_map/while/body/eval_jaxpr/ppermute | solution.py:18
  204.6 6.0 collective-permute-start.1
  212.8 15.3 %collective-permute-start = (bf16[128,2,128]{2,0,1:T(8,128)(2,1)S(1)}, bf16[128,2,128]{2,0,1:T(8,128)(2,1)S(1)}, u32[]{:S(2)}, u32[]{:S(2)}) collective-permute-start(bf16[128,2,128]{2,0,1:T(8,128)(2,1)S(1)} %copy.108), channel_id=1, source_target_pairs={{0,8},{8,16},{16,24},{24,32},{32,40},{40,48},{48,56},{56,64},{64,7... | collective-permute-start | bytes 196616 | tf_op jit(solution)/shard_map/while/body/eval_jaxpr/ppermute | solution.py:18
  217.7 10.5 %collective-permute-start.1 = (bf16[128,2,128]{2,0,1:T(8,128)(2,1)S(1)}, bf16[128,2,128]{2,0,1:T(8,128)(2,1)}, u32[]{:S(2)}, u32[]{:S(2)}) collective-permute-start(bf16[128,2,128]{2,0,1:T(8,128)(2,1)S(1)} %copy.109), channel_id=1, source_target_pairs={{0,8},{8,16},{16,24},{24,32},{32,40},{40,48},{48,56},{56,64},{64,7... | collective-permute-start | bytes 196616 | tf_op jit(solution)/shard_map/while/body/eval_jaxpr/ppermute | solution.py:18
  222.4 6.9 %collective-permute-start.2 = (f32[128,2,128]{2,0,1:T(8,128)S(1)}, f32[128,2,128]{2,0,1:T(8,128)S(1)}, u32[]{:S(2)}, u32[]{:S(2)}) collective-permute-start(f32[128,2,128]{2,0,1:T(8,128)S(1)} %fusion.151), channel_id=1, source_target_pairs={{0,8},{8,16},{16,24},{24,32},{32,40},{40,48},{48,56},{56,64},{64,7... | collective-permute-start | bytes 393224 | tf_op jit(solution)/shard_map/while/body/eval_jaxpr/ppermute | solution.py:18
  230.7 10.6 %collective-permute-start = (bf16[128,2,128]{2,0,1:T(8,128)(2,1)S(1)}, bf16[128,2,128]{2,0,1:T(8,128)(2,1)S(1)}, u32[]{:S(2)}, u32[]{:S(2)}) collective-permute-start(bf16[128,2,128]{2,0,1:T(8,128)(2,1)S(1)} %copy.108), channel_id=1, source_target_pairs={{0,8},{8,16},{16,24},{24,32},{32,40},{40,48},{48,56},{56,64},{64,7... | collective-permute-start | bytes 196616 | tf_op jit(solution)/shard_map/while/body/eval_jaxpr/ppermute | solution.py:18
  235.5 5.7 collective-permute-start.1
  243.7 9.6 %collective-permute-start = (bf16[128,2,128]{2,0,1:T(8,128)(2,1)S(1)}, bf16[128,2,128]{2,0,1:T(8,128)(2,1)S(1)}, u32[]{:S(2)}, u32[]{:S(2)}) collective-permute-start(bf16[128,2,128]{2,0,1:T(8,128)(2,1)S(1)} %copy.108), channel_id=1, source_target_pairs={{0,8},{8,16},{16,24},{24,32},{32,40},{40,48},{48,56},{56,64},{64,7... | collective-permute-start | bytes 196616 | tf_op jit(solution)/shard_map/while/body/eval_jaxpr/ppermute | solution.py:18
  255.8 10.0 %collective-permute-start = (bf16[128,2,128]{2,0,1:T(8,128)(2,1)S(1)}, bf16[128,2,128]{2,0,1:T(8,128)(2,1)S(1)}, u32[]{:S(2)}, u32[]{:S(2)}) collective-permute-start(bf16[128,2,128]{2,0,1:T(8,128)(2,1)S(1)} %copy.108), channel_id=1, source_target_pairs={{0,8},{8,16},{16,24},{24,32},{32,40},{40,48},{48,56},{56,64},{64,7... | collective-permute-start | bytes 196616 | tf_op jit(solution)/shard_map/while/body/eval_jaxpr/ppermute | solution.py:18
  268.3 10.3 %collective-permute-start = (bf16[128,2,128]{2,0,1:T(8,128)(2,1)S(1)}, bf16[128,2,128]{2,0,1:T(8,128)(2,1)S(1)}, u32[]{:S(2)}, u32[]{:S(2)}) collective-permute-start(bf16[128,2,128]{2,0,1:T(8,128)(2,1)S(1)} %copy.108), channel_id=1, source_target_pairs={{0,8},{8,16},{16,24},{24,32},{32,40},{40,48},{48,56},{56,64},{64,7... | collective-permute-start | bytes 196616 | tf_op jit(solution)/shard_map/while/body/eval_jaxpr/ppermute | solution.py:18
  281.1 9.7 %collective-permute-start = (bf16[128,2,128]{2,0,1:T(8,128)(2,1)S(1)}, bf16[128,2,128]{2,0,1:T(8,128)(2,1)S(1)}, u32[]{:S(2)}, u32[]{:S(2)}) collective-permute-start(bf16[128,2,128]{2,0,1:T(8,128)(2,1)S(1)} %copy.108), channel_id=1, source_target_pairs={{0,8},{8,16},{16,24},{24,32},{32,40},{40,48},{48,56},{56,64},{64,7... | collective-permute-start | bytes 196616 | tf_op jit(solution)/shard_map/while/body/eval_jaxpr/ppermute | solution.py:18
  293.3 10.6 %collective-permute-start = (bf16[128,2,128]{2,0,1:T(8,128)(2,1)S(1)}, bf16[128,2,128]{2,0,1:T(8,128)(2,1)S(1)}, u32[]{:S(2)}, u32[]{:S(2)}) collective-permute-start(bf16[128,2,128]{2,0,1:T(8,128)(2,1)S(1)} %copy.108), channel_id=1, source_target_pairs={{0,8},{8,16},{16,24},{24,32},{32,40},{40,48},{48,56},{56,64},{64,7... | collective-permute-start | bytes 196616 | tf_op jit(solution)/shard_map/while/body/eval_jaxpr/ppermute | solution.py:18
  298.1 5.8 collective-permute-start.1
  306.4 10.7 %collective-permute-start = (bf16[128,2,128]{2,0,1:T(8,128)(2,1)S(1)}, bf16[128,2,128]{2,0,1:T(8,128)(2,1)S(1)}, u32[]{:S(2)}, u32[]{:S(2)}) collective-permute-start(bf16[128,2,128]{2,0,1:T(8,128)(2,1)S(1)} %copy.108), channel_id=1, source_target_pairs={{0,8},{8,16},{16,24},{24,32},{32,40},{40,48},{48,56},{56,64},{64,7... | collective-permute-start | bytes 196616 | tf_op jit(solution)/shard_map/while/body/eval_jaxpr/ppermute | solution.py:18
  311.2 5.9 collective-permute-start.1
  319.6 9.3 %collective-permute-start = (bf16[128,2,128]{2,0,1:T(8,128)(2,1)S(1)}, bf16[128,2,128]{2,0,1:T(8,128)(2,1)S(1)}, u32[]{:S(2)}, u32[]{:S(2)}) collective-permute-start(bf16[128,2,128]{2,0,1:T(8,128)(2,1)S(1)} %copy.108), channel_id=1, source_target_pairs={{0,8},{8,16},{16,24},{24,32},{32,40},{40,48},{48,56},{56,64},{64,7... | collective-permute-start | bytes 196616 | tf_op jit(solution)/shard_map/while/body/eval_jaxpr/ppermute | solution.py:18
  331.4 12.0 %collective-permute-start = (bf16[128,2,128]{2,0,1:T(8,128)(2,1)S(1)}, bf16[128,2,128]{2,0,1:T(8,128)(2,1)S(1)}, u32[]{:S(2)}, u32[]{:S(2)}) collective-permute-start(bf16[128,2,128]{2,0,1:T(8,128)(2,1)S(1)} %copy.108), channel_id=1, source_target_pairs={{0,8},{8,16},{16,24},{24,32},{32,40},{40,48},{48,56},{56,64},{64,7... | collective-permute-start | bytes 196616 | tf_op jit(solution)/shard_map/while/body/eval_jaxpr/ppermute | solution.py:18
  336.2 7.2 %collective-permute-start.1 = (bf16[128,2,128]{2,0,1:T(8,128)(2,1)S(1)}, bf16[128,2,128]{2,0,1:T(8,128)(2,1)}, u32[]{:S(2)}, u32[]{:S(2)}) collective-permute-start(bf16[128,2,128]{2,0,1:T(8,128)(2,1)S(1)} %copy.109), channel_id=1, source_target_pairs={{0,8},{8,16},{16,24},{24,32},{32,40},{40,48},{48,56},{56,64},{64,7... | collective-permute-start | bytes 196616 | tf_op jit(solution)/shard_map/while/body/eval_jaxpr/ppermute | solution.py:18
  337.7 6.8 %collective-permute-start.2 = (f32[128,2,128]{2,0,1:T(8,128)S(1)}, f32[128,2,128]{2,0,1:T(8,128)S(1)}, u32[]{:S(2)}, u32[]{:S(2)}) collective-permute-start(f32[128,2,128]{2,0,1:T(8,128)S(1)} %fusion.151), channel_id=1, source_target_pairs={{0,8},{8,16},{16,24},{24,32},{32,40},{40,48},{48,56},{56,64},{64,7... | collective-permute-start | bytes 393224 | tf_op jit(solution)/shard_map/while/body/eval_jaxpr/ppermute | solution.py:18
  345.9 9.3 %collective-permute-start = (bf16[128,2,128]{2,0,1:T(8,128)(2,1)S(1)}, bf16[128,2,128]{2,0,1:T(8,128)(2,1)S(1)}, u32[]{:S(2)}, u32[]{:S(2)}) collective-permute-start(bf16[128,2,128]{2,0,1:T(8,128)(2,1)S(1)} %copy.108), channel_id=1, source_target_pairs={{0,8},{8,16},{16,24},{24,32},{32,40},{40,48},{48,56},{56,64},{64,7... | collective-permute-start | bytes 196616 | tf_op jit(solution)/shard_map/while/body/eval_jaxpr/ppermute | solution.py:18
  357.7 9.7 %collective-permute-start = (bf16[128,2,128]{2,0,1:T(8,128)(2,1)S(1)}, bf16[128,2,128]{2,0,1:T(8,128)(2,1)S(1)}, u32[]{:S(2)}, u32[]{:S(2)}) collective-permute-start(bf16[128,2,128]{2,0,1:T(8,128)(2,1)S(1)} %copy.108), channel_id=1, source_target_pairs={{0,8},{8,16},{16,24},{24,32},{32,40},{40,48},{48,56},{56,64},{64,7... | collective-permute-start | bytes 196616 | tf_op jit(solution)/shard_map/while/body/eval_jaxpr/ppermute | solution.py:18
  369.9 9.3 %collective-permute-start = (bf16[128,2,128]{2,0,1:T(8,128)(2,1)S(1)}, bf16[128,2,128]{2,0,1:T(8,128)(2,1)S(1)}, u32[]{:S(2)}, u32[]{:S(2)}) collective-permute-start(bf16[128,2,128]{2,0,1:T(8,128)(2,1)S(1)} %copy.108), channel_id=1, source_target_pairs={{0,8},{8,16},{16,24},{24,32},{32,40},{40,48},{48,56},{56,64},{64,7... | collective-permute-start | bytes 196616 | tf_op jit(solution)/shard_map/while/body/eval_jaxpr/ppermute | solution.py:18
  381.7 9.9 %collective-permute-start = (bf16[128,2,128]{2,0,1:T(8,128)(2,1)S(1)}, bf16[128,2,128]{2,0,1:T(8,128)(2,1)S(1)}, u32[]{:S(2)}, u32[]{:S(2)}) collective-permute-start(bf16[128,2,128]{2,0,1:T(8,128)(2,1)S(1)} %copy.108), channel_id=1, source_target_pairs={{0,8},{8,16},{16,24},{24,32},{32,40},{40,48},{48,56},{56,64},{64,7... | collective-permute-start | bytes 196616 | tf_op jit(solution)/shard_map/while/body/eval_jaxpr/ppermute | solution.py:18
  394.1 9.8 %collective-permute-start = (bf16[128,2,128]{2,0,1:T(8,128)(2,1)S(1)}, bf16[128,2,128]{2,0,1:T(8,128)(2,1)S(1)}, u32[]{:S(2)}, u32[]{:S(2)}) collective-permute-start(bf16[128,2,128]{2,0,1:T(8,128)(2,1)S(1)} %copy.108), channel_id=1, source_target_pairs={{0,8},{8,16},{16,24},{24,32},{32,40},{40,48},{48,56},{56,64},{64,7... | collective-permute-start | bytes 196616 | tf_op jit(solution)/shard_map/while/body/eval_jaxpr/ppermute | solution.py:18
  406.4 10.6 %collective-permute-start = (bf16[128,2,128]{2,0,1:T(8,128)(2,1)S(1)}, bf16[128,2,128]{2,0,1:T(8,128)(2,1)S(1)}, u32[]{:S(2)}, u32[]{:S(2)}) collective-permute-start(bf16[128,2,128]{2,0,1:T(8,128)(2,1)S(1)} %copy.108), channel_id=1, source_target_pairs={{0,8},{8,16},{16,24},{24,32},{32,40},{40,48},{48,56},{56,64},{64,7... | collective-permute-start | bytes 196616 | tf_op jit(solution)/shard_map/while/body/eval_jaxpr/ppermute | solution.py:18
  411.2 5.8 collective-permute-start.1
  419.5 9.3 %collective-permute-start = (bf16[128,2,128]{2,0,1:T(8,128)(2,1)S(1)}, bf16[128,2,128]{2,0,1:T(8,128)(2,1)S(1)}, u32[]{:S(2)}, u32[]{:S(2)}) collective-permute-start(bf16[128,2,128]{2,0,1:T(8,128)(2,1)S(1)} %copy.108), channel_id=1, source_target_pairs={{0,8},{8,16},{16,24},{24,32},{32,40},{40,48},{48,56},{56,64},{64,7... | collective-permute-start | bytes 196616 | tf_op jit(solution)/shard_map/while/body/eval_jaxpr/ppermute | solution.py:18
  431.3 9.6 %collective-permute-start = (bf16[128,2,128]{2,0,1:T(8,128)(2,1)S(1)}, bf16[128,2,128]{2,0,1:T(8,128)(2,1)S(1)}, u32[]{:S(2)}, u32[]{:S(2)}) collective-permute-start(bf16[128,2,128]{2,0,1:T(8,128)(2,1)S(1)} %copy.108), channel_id=1, source_target_pairs={{0,8},{8,16},{16,24},{24,32},{32,40},{40,48},{48,56},{56,64},{64,7... | collective-permute-start | bytes 196616 | tf_op jit(solution)/shard_map/while/body/eval_jaxpr/ppermute | solution.py:18
  443.4 9.6 %collective-permute-start = (bf16[128,2,128]{2,0,1:T(8,128)(2,1)S(1)}, bf16[128,2,128]{2,0,1:T(8,128)(2,1)S(1)}, u32[]{:S(2)}, u32[]{:S(2)}) collective-permute-start(bf16[128,2,128]{2,0,1:T(8,128)(2,1)S(1)} %copy.108), channel_id=1, source_target_pairs={{0,8},{8,16},{16,24},{24,32},{32,40},{40,48},{48,56},{56,64},{64,7... | collective-permute-start | bytes 196616 | tf_op jit(solution)/shard_map/while/body/eval_jaxpr/ppermute | solution.py:18
  455.5 10.0 %collective-permute-start = (bf16[128,2,128]{2,0,1:T(8,128)(2,1)S(1)}, bf16[128,2,128]{2,0,1:T(8,128)(2,1)S(1)}, u32[]{:S(2)}, u32[]{:S(2)}) collective-permute-start(bf16[128,2,128]{2,0,1:T(8,128)(2,1)S(1)} %copy.108), channel_id=1, source_target_pairs={{0,8},{8,16},{16,24},{24,32},{32,40},{40,48},{48,56},{56,64},{64,7... | collective-permute-start | bytes 196616 | tf_op jit(solution)/shard_map/while/body/eval_jaxpr/ppermute | solution.py:18
  467.9 10.3 %collective-permute-start = (bf16[128,2,128]{2,0,1:T(8,128)(2,1)S(1)}, bf16[128,2,128]{2,0,1:T(8,128)(2,1)S(1)}, u32[]{:S(2)}, u32[]{:S(2)}) collective-permute-start(bf16[128,2,128]{2,0,1:T(8,128)(2,1)S(1)} %copy.108), channel_id=1, source_target_pairs={{0,8},{8,16},{16,24},{24,32},{32,40},{40,48},{48,56},{56,64},{64,7... | collective-permute-start | bytes 196616 | tf_op jit(solution)/shard_map/while/body/eval_jaxpr/ppermute | solution.py:18
  480.8 9.7 %collective-permute-start = (bf16[128,2,128]{2,0,1:T(8,128)(2,1)S(1)}, bf16[128,2,128]{2,0,1:T(8,128)(2,1)S(1)}, u32[]{:S(2)}, u32[]{:S(2)}) collective-permute-start(bf16[128,2,128]{2,0,1:T(8,128)(2,1)S(1)} %copy.108), channel_id=1, source_target_pairs={{0,8},{8,16},{16,24},{24,32},{32,40},{40,48},{48,56},{56,64},{64,7... | collective-permute-start | bytes 196616 | tf_op jit(solution)/shard_map/while/body/eval_jaxpr/ppermute | solution.py:18
  493.0 10.6 %collective-permute-start = (bf16[128,2,128]{2,0,1:T(8,128)(2,1)S(1)}, bf16[128,2,128]{2,0,1:T(8,128)(2,1)S(1)}, u32[]{:S(2)}, u32[]{:S(2)}) collective-permute-start(bf16[128,2,128]{2,0,1:T(8,128)(2,1)S(1)} %copy.108), channel_id=1, source_target_pairs={{0,8},{8,16},{16,24},{24,32},{32,40},{40,48},{48,56},{56,64},{64,7... | collective-permute-start | bytes 196616 | tf_op jit(solution)/shard_map/while/body/eval_jaxpr/ppermute | solution.py:18
  497.8 5.8 collective-permute-start.1
  506.1 10.7 %collective-permute-start = (bf16[128,2,128]{2,0,1:T(8,128)(2,1)S(1)}, bf16[128,2,128]{2,0,1:T(8,128)(2,1)S(1)}, u32[]{:S(2)}, u32[]{:S(2)}) collective-permute-start(bf16[128,2,128]{2,0,1:T(8,128)(2,1)S(1)} %copy.108), channel_id=1, source_target_pairs={{0,8},{8,16},{16,24},{24,32},{32,40},{40,48},{48,56},{56,64},{64,7... | collective-permute-start | bytes 196616 | tf_op jit(solution)/shard_map/while/body/eval_jaxpr/ppermute | solution.py:18
  510.9 5.9 collective-permute-start.1
  519.3 9.3 %collective-permute-start = (bf16[128,2,128]{2,0,1:T(8,128)(2,1)S(1)}, bf16[128,2,128]{2,0,1:T(8,128)(2,1)S(1)}, u32[]{:S(2)}, u32[]{:S(2)}) collective-permute-start(bf16[128,2,128]{2,0,1:T(8,128)(2,1)S(1)} %copy.108), channel_id=1, source_target_pairs={{0,8},{8,16},{16,24},{24,32},{32,40},{40,48},{48,56},{56,64},{64,7... | collective-permute-start | bytes 196616 | tf_op jit(solution)/shard_map/while/body/eval_jaxpr/ppermute | solution.py:18
  531.1 12.0 %collective-permute-start = (bf16[128,2,128]{2,0,1:T(8,128)(2,1)S(1)}, bf16[128,2,128]{2,0,1:T(8,128)(2,1)S(1)}, u32[]{:S(2)}, u32[]{:S(2)}) collective-permute-start(bf16[128,2,128]{2,0,1:T(8,128)(2,1)S(1)} %copy.108), channel_id=1, source_target_pairs={{0,8},{8,16},{16,24},{24,32},{32,40},{40,48},{48,56},{56,64},{64,7... | collective-permute-start | bytes 196616 | tf_op jit(solution)/shard_map/while/body/eval_jaxpr/ppermute | solution.py:18
  535.9 7.2 %collective-permute-start.1 = (bf16[128,2,128]{2,0,1:T(8,128)(2,1)S(1)}, bf16[128,2,128]{2,0,1:T(8,128)(2,1)}, u32[]{:S(2)}, u32[]{:S(2)}) collective-permute-start(bf16[128,2,128]{2,0,1:T(8,128)(2,1)S(1)} %copy.109), channel_id=1, source_target_pairs={{0,8},{8,16},{16,24},{24,32},{32,40},{40,48},{48,56},{56,64},{64,7... | collective-permute-start | bytes 196616 | tf_op jit(solution)/shard_map/while/body/eval_jaxpr/ppermute | solution.py:18
  537.4 6.8 %collective-permute-start.2 = (f32[128,2,128]{2,0,1:T(8,128)S(1)}, f32[128,2,128]{2,0,1:T(8,128)S(1)}, u32[]{:S(2)}, u32[]{:S(2)}) collective-permute-start(f32[128,2,128]{2,0,1:T(8,128)S(1)} %fusion.151), channel_id=1, source_target_pairs={{0,8},{8,16},{16,24},{24,32},{32,40},{40,48},{48,56},{56,64},{64,7... | collective-permute-start | bytes 393224 | tf_op jit(solution)/shard_map/while/body/eval_jaxpr/ppermute | solution.py:18
  545.6 9.3 %collective-permute-start = (bf16[128,2,128]{2,0,1:T(8,128)(2,1)S(1)}, bf16[128,2,128]{2,0,1:T(8,128)(2,1)S(1)}, u32[]{:S(2)}, u32[]{:S(2)}) collective-permute-start(bf16[128,2,128]{2,0,1:T(8,128)(2,1)S(1)} %copy.108), channel_id=1, source_target_pairs={{0,8},{8,16},{16,24},{24,32},{32,40},{40,48},{48,56},{56,64},{64,7... | collective-permute-start | bytes 196616 | tf_op jit(solution)/shard_map/while/body/eval_jaxpr/ppermute | solution.py:18
  557.4 9.7 %collective-permute-start = (bf16[128,2,128]{2,0,1:T(8,128)(2,1)S(1)}, bf16[128,2,128]{2,0,1:T(8,128)(2,1)S(1)}, u32[]{:S(2)}, u32[]{:S(2)}) collective-permute-start(bf16[128,2,128]{2,0,1:T(8,128)(2,1)S(1)} %copy.108), channel_id=1, source_target_pairs={{0,8},{8,16},{16,24},{24,32},{32,40},{40,48},{48,56},{56,64},{64,7... | collective-permute-start | bytes 196616 | tf_op jit(solution)/shard_map/while/body/eval_jaxpr/ppermute | solution.py:18
  569.6 9.3 %collective-permute-start = (bf16[128,2,128]{2,0,1:T(8,128)(2,1)S(1)}, bf16[128,2,128]{2,0,1:T(8,128)(2,1)S(1)}, u32[]{:S(2)}, u32[]{:S(2)}) collective-permute-start(bf16[128,2,128]{2,0,1:T(8,128)(2,1)S(1)} %copy.108), channel_id=1, source_target_pairs={{0,8},{8,16},{16,24},{24,32},{32,40},{40,48},{48,56},{56,64},{64,7... | collective-permute-start | bytes 196616 | tf_op jit(solution)/shard_map/while/body/eval_jaxpr/ppermute | solution.py:18
  581.4 9.9 %collective-permute-start = (bf16[128,2,128]{2,0,1:T(8,128)(2,1)S(1)}, bf16[128,2,128]{2,0,1:T(8,128)(2,1)S(1)}, u32[]{:S(2)}, u32[]{:S(2)}) collective-permute-start(bf16[128,2,128]{2,0,1:T(8,128)(2,1)S(1)} %copy.108), channel_id=1, source_target_pairs={{0,8},{8,16},{16,24},{24,32},{32,40},{40,48},{48,56},{56,64},{64,7... | collective-permute-start | bytes 196616 | tf_op jit(solution)/shard_map/while/body/eval_jaxpr/ppermute | solution.py:18
  596.8 6.8 %collective-permute-start.4 = (f32[128,2,128]{2,0,1:T(8,128)S(1)}, f32[128,2,128]{2,0,1:T(8,128)S(1)}, u32[]{:S(2)}, u32[]{:S(2)}) collective-permute-start(f32[128,2,128]{2,0,1:T(8,128)S(1)} %fusion.49), channel_id=1, source_target_pairs={{0,8},{8,16},{16,24},{24,32},{32,40},{40,48},{48,56},{56,64},{64,7... | collective-permute-start | bytes 393224 | tf_op jit(solution)/shard_map/ppermute | solution.py:18
  614.8 7.6 %collective-permute-start.6 = (bf16[64,3584]{1,0:T(8,128)(2,1)S(1)}, bf16[64,3584]{1,0:T(8,128)(2,1)S(1)}, u32[]{:S(2)}, u32[]{:S(2)}) collective-permute-start(bf16[64,3584]{1,0:T(8,128)(2,1)S(1)} %get-tuple-element.694), channel_id=1, source_target_pairs={{0,8},{8,0},{16,24},{24,16},{32,40},{40,32},{48,56},{56,48},{64,72... | collective-permute-start | bytes 1376264 | tf_op jit(solution)/shard_map/ppermute | solution.py:26
  (96 other events, 561.1 us)
Sparse Core Ops, SparseCore 0:
  10.8 84.0 all-gather.2
  97.6 132.6 all-gather.4
where the time goes:
time: 640 us; the launch traced here: 636 us
  starting transfers between devices  229 us (36%)
  waiting for transfers between devices  155 us (24%)
  matrix products  94.1 us (15%)
  local copies, waits for them, and re-layouts  90.5 us (14%)
  loops' own time  25.2 us (4%)
  other arithmetic  23.4 us (4%)
  between operations  18.9 us (3%)
    ppermute x126, starting transfers between devices, shifted(): return lax.ppermute(value, axis, pairs)  223 us
    ppermute x126, waiting for transfers between devices, shifted(): return lax.ppermute(value, axis, pairs)  78.3 us
    all_gather x1, waiting for transfers between devices, body(): key_piece = lax.all_gather(keys, 'seq', axis=0, tiled=True)  75.1 us
    dynamic_slice x64, local copies, waits for them, and re-layouts, body(): lax.scan(absorb, zero_stats, (stacked, jnp.arange(shards, dtype=jnp.int32)))  48.1 us
    while x94, local copies, waits for them, and re-layouts  26.3 us
    another operation x1, loops' own time, body(): lax.scan(absorb, zero_stats, (stacked, jnp.arange(shards, dtype=jnp.int32)))  22.9 us
    dot_general x64, matrix products, score_block(): jnp.einsum('qkgd,tkd->kgqt', query_part, keys_here, preferred_element_typ...  20.6 us
    dot_general x64, matrix products, key_mask(): allowed = jnp.dot(query_live, key_onehot.T)  16.3 us
  transfers between devices with their start and end apart: 129, of which 64 were waited for; matrix products, arithmetic and copies ran while one was open for 30% of the time, Pallas kernels for 0%

commit v1 on v0

v1 whole, which is shorter than its diff:
```python
import jax
import jax.numpy as jnp
from jax import lax
from jax.experimental import pallas as pl
from jax.experimental.pallas import tpu as pltpu
from jax.sharding import PartitionSpec as P

HG = 7
HD = 128
GW = 896
CW = 1152
D = 3584
WR = 112
EPSILON = 1e-06
LOG2E = 1.4426950408889634
SCALE = 128 ** -0.5
TILE = 256
BF = jnp.bfloat16
F32 = jnp.float32
MESH = pl.DeviceIdType.MESH


class Place:
    def __init__(self):
        s = lax.axis_index("seq")
        b = lax.axis_index("batch")
        self.s = s
        self.c = s % 2
        self.h = (s // 2) % 2
        self.z = s // 4
        self.l = b % 2
        self.x = b // 2
        self.unit = (self.x + 2 * self.l) % 4

    def dev(self, dz=0, h=None, c=None, dx=0, l=None):
        z = (self.z + dz + 8) % 8
        x = (self.x + dx + 4) % 4
        h = self.h if h is None else h
        c = self.c if c is None else c
        l = self.l if l is None else l
        return {"seq": (z * 2 + h) * 2 + c, "batch": x * 2 + l}

    def chip(self, dz, h):
        return ((self.z + dz + 8) % 8) * 2 + h


class Links:
    def __init__(self, send, recv):
        self.send, self.recv, self.used = send, recv, 0

    def copy(self, src, dst, dev):
        i = self.used
        self.used += 1
        return pltpu.make_async_remote_copy(
            src_ref=src, dst_ref=dst, send_sem=self.send.at[i], recv_sem=self.recv.at[i],
            device_id=dev, device_id_type=MESH)


def greet(devs):
    barrier = pltpu.get_barrier_semaphore()
    for d in devs:
        pl.semaphore_signal(barrier, inc=1, device_id=d, device_id_type=MESH)
    pl.semaphore_wait(barrier, len(devs))


def weight_parts(half):
    return ((half * GW, GW, 0), (HG * 2 * HD + half * HD, HD, GW), (HG * 2 * HD + 2 * HD + half * HD, HD, GW + HD))


IN_LINKS = 96
LEVELS = 5


def gather_kernel(k_ref, v_ref, q_ref, do_ref, dl_ref, w_ref, kvg, q2, do2, dl2, wg, w2, away, wu, w0, send, recv, loc):
    p = Place()
    links = Links(send, recv)
    partner = p.dev(c=1 - p.c)
    across = [p.dev(h=1 - p.h, l=1 - p.l, c=0), p.dev(h=1 - p.h, l=1 - p.l, c=1)]
    ypeer = p.dev(h=1 - p.h)
    zs = {1: p.dev(dz=1), -1: p.dev(dz=-1)}
    fan = [p.dev(dx=1), p.dev(dx=-1), p.dev(l=1 - p.l)]
    mine, other = p.c, 1 - p.c
    col = lambda i, w: pl.ds(pl.multiple_of(i * w, 128), w)
    sent = []
    own = [pltpu.make_async_copy(k_ref.at[:, col(mine, HD)], kvg.at[p.s, 0], loc.at[0]),
           pltpu.make_async_copy(v_ref.at[:, col(mine, HD)], kvg.at[p.s, 1], loc.at[1])]
    pack = [pltpu.make_async_copy(k_ref.at[:, col(other, HD)], away.at[0], loc.at[2]),
            pltpu.make_async_copy(v_ref.at[:, col(other, HD)], away.at[1], loc.at[3])]
    rest = [pltpu.make_async_copy(q_ref.at[:, col(mine, GW)], q2.at[p.c], loc.at[4]),
            pltpu.make_async_copy(do_ref.at[:, col(mine, GW)], do2.at[p.c], loc.at[5]),
            pltpu.make_async_copy(dl_ref.at[mine], dl2.at[p.c], loc.at[6])]
    for cp in own + pack + rest:
        cp.start()
    greet([partner, ypeer] + across + [zs[1], zs[-1]] + fan)

    def begin(cp):
        cp.start()
        sent.append(cp)
        return cp

    swap = links.copy(away, kvg.at[p.s], partner)
    for cp in pack:
        cp.wait()
    begin(swap)
    for cp in own:
        cp.wait()
    kv = {}
    slot = lambda dz, e, q: 2 * p.chip(dz, p.h if e == 0 else 1 - p.h) + (p.c if q == 0 else 1 - p.c)

    def kv_send(step, e, q, dr):
        block = kvg.at[slot(-dr * (step - 1), e, q)]
        kv[step, e, q, dr] = begin(links.copy(block, block, zs[dr]))

    def y_send(q):
        block = kvg.at[slot(0, 0, q)]
        return begin(links.copy(block, block, ypeer))

    sy = {0: y_send(0)}
    for dr in (1, -1):
        kv_send(1, 0, 0, dr)

    lead = p.unit % 2 == p.c
    to_partner, to_self, to_across = [], [], []
    for i, (start, width, at) in enumerate(weight_parts(other)):
        to_partner.append(links.copy(w_ref.at[:, pl.ds(pl.multiple_of(start, 128), width)],
                                     w0.at[2 * p.h + p.c, :, pl.ds(at, width)], partner))
    for i, (start, width, at) in enumerate(weight_parts(mine)):
        to_self.append(pltpu.make_async_copy(w_ref.at[:, pl.ds(pl.multiple_of(start, 128), width)],
                                             w0.at[2 * p.h + p.c, :, pl.ds(at, width)], loc.at[7 + i]))
    for half in (0, 1):
        for i, (start, width, at) in enumerate(weight_parts(half)):
            n = links.used
            links.used += 1
            to_across.append((p.c, half, i, w_ref.at[:, pl.ds(start, width)], w0.at[2 * p.h + p.c, :, pl.ds(at, width)], n))
    first = IN_LINKS - 6
    to_across = [pltpu.make_async_remote_copy(
        src_ref=src, dst_ref=dst, send_sem=send.at[n], recv_sem=recv.at[first + 3 * d + i],
        device_id=across[half], device_id_type=MESH) for d, half, i, src, dst, n in to_across]
    from_across = [[pltpu.make_async_remote_copy(
        src_ref=w_ref.at[:, pl.ds(start, width)], dst_ref=w0.at[2 * (1 - p.h) + d, :, pl.ds(at, width)],
        send_sem=send.at[0], recv_sem=recv.at[first + 3 * d + i],
        device_id=across[0], device_id_type=MESH) for i, (start, width, at) in enumerate(weight_parts(0))] for d in (0, 1)]
    for cp in to_self:
        cp.start()
    for cp in to_partner:
        begin(cp)

    @pl.when(lead)
    def _():
        for cp in to_across:
            cp.start()

    swap.wait_recv()
    sy[1] = y_send(1)
    for dr in (1, -1):
        kv_send(1, 0, 1, dr)

    side = [links.copy(q_ref.at[:, col(other, GW)], q2.at[p.c], partner),
            links.copy(do_ref.at[:, col(other, GW)], do2.at[p.c], partner),
            links.copy(dl_ref.at[other], dl2.at[p.c], partner)]
    for cp in side:
        begin(cp)
    for q in (0, 1):
        sy[q].wait_recv()
        for dr in (1, -1):
            kv_send(1, 1, q, dr)

    wz, fans, keep = {}, {}, []

    def store(src, dst):
        cp = pltpu.make_async_copy(src, dst, loc.at[10 + len(keep)])
        cp.start()
        keep.append(cp)

    def w_send(step):
        for dr in (1, -1):
            src = w0.at[p.unit] if step == 1 else wu.at[2 - dr * (step - 1)]
            wz[step, dr] = begin(links.copy(src, wu.at[2 - dr * step], zs[dr]))

    def w_take(step):
        for dr in (1, -1):
            wz[step, dr].wait_recv()
        if step == 1:
            w_send(2)
            for dr in (1, -1):
                for n, dev in enumerate(fan):
                    fans[dr, n] = begin(links.copy(wu.at[2 - dr], wg.at[1 - dr, 1 + n], dev))
                store(wu.at[2 - dr], wg.at[1 - dr, 0])
        else:
            for dr in (1, -1):
                store(wu.at[2 - 2 * dr], w2.at[(1 - dr) // 2])

    def kv_step(step, e):
        for q in (0, 1):
            for dr in (1, -1):
                kv[step, e, q, dr].wait_recv()
                if step < 3 or (dr == 1) == (e == 0):
                    kv_send(step + 1, e, q, dr)

    for cp in to_self:
        cp.wait()
    for cp in to_partner:
        cp.wait_recv()

    for d in (0, 1):
        @pl.when(p.unit % 2 == d)
        def _():
            for cp in from_across[d]:
                cp.wait_recv()
    w_send(1)
    kv_step(1, 0)

    @pl.when(jnp.logical_not(lead))
    def _():
        for cp in to_across:
            cp.start()
    kv_step(1, 1)
    kv_step(2, 0)
    w_take(1)
    kv_step(2, 1)
    kv_step(3, 0)
    w_take(2)
    kv_step(3, 1)
    for d in (0, 1):
        @pl.when(p.unit % 2 != d)
        def _():
            for cp in from_across[d]:
                cp.wait_recv()
    for n, turn in enumerate((0, 3, 1, 2)):
        store(w0.at[(p.unit + turn) % 4], wg.at[1, n])
    for q in (0, 1):
        kv[4, 0, q, 1].wait_recv()
        kv[4, 1, q, -1].wait_recv()
    for cp in fans.values():
        cp.wait_recv()
    for cp in rest + keep:
        cp.wait()
    for cp in side:
        cp.wait_recv()
    for cp in sent:
        cp.wait_send()

    for cp in to_across:
        cp.wait_send()


def gather(keys, values, queries, out_grad, delta, weight):
    hbm = pl.BlockSpec(memory_space=pl.ANY)
    vmem = pl.BlockSpec(memory_space=pltpu.VMEM)
    return pl.pallas_call(
        gather_kernel,
        out_shape=(jax.ShapeDtypeStruct((32, 2, 128, HD), BF), jax.ShapeDtypeStruct((2, 128, GW), BF),
                   jax.ShapeDtypeStruct((2, 128, GW), BF), jax.ShapeDtypeStruct((2, 8, 128), F32),
                   jax.ShapeDtypeStruct((3, 4, WR, CW), BF), jax.ShapeDtypeStruct((2, WR, CW), BF)),
        in_specs=[hbm] * 6,
        out_specs=(vmem, vmem, vmem, vmem, hbm, hbm),
        scratch_shapes=[pltpu.VMEM((2, 128, HD), BF), pltpu.VMEM((LEVELS, WR, CW), BF), pltpu.VMEM((4, WR, CW), BF),
                        pltpu.SemaphoreType.DMA((IN_LINKS,)), pltpu.SemaphoreType.DMA((IN_LINKS,)),
                        pltpu.SemaphoreType.DMA((24,))],
        compiler_params=pltpu.CompilerParams(collective_id=0, has_side_effects=True),
        name="gather",
    )(keys, values, queries, out_grad, delta, weight)


def attn_kernel(order_ref, mask_ref, q_ref, do_ref, delta_ref, kv_ref, dq_ref, dkv_ref,
                inv_ref, live_ref, dks, dvs, qs, qt, dos, dot_, m_ref, l_ref, dl_ref, dqt):
    chip = lax.axis_index("seq") // 2

    def invert(i, _):
        inv_ref[order_ref[i]] = i
        return 0
    lax.fori_loop(0, 64, invert, 0, unroll=8)
    dks[...] = jnp.zeros_like(dks)
    dvs[...] = jnp.zeros_like(dvs)
    qs[HG * 64:, :] = jnp.zeros((64, HD), BF)
    dos[HG * 64:, :] = jnp.zeros((64, HD), BF)
    lane8 = lax.broadcasted_iota(jnp.int32, (1, 128), 1)
    ahead = lax.broadcasted_iota(jnp.int32, (64, 128), 0) - lax.broadcasted_iota(jnp.int32, (64, 128), 1) % 64

    def query_block(i, _):
        block = order_ref[4 * chip + i]
        dev, odd = i // 2, i % 2
        half = pl.multiple_of(odd * 64, 64)
        for src, st, tr in ((q_ref, qs, qt), (do_ref, dos, dot_)):
            for h in range(HG):
                st[h * 64:(h + 1) * 64, :] = src[dev, pl.ds(half, 64), h * HD:(h + 1) * HD]
            for r in range(4):
                tr[:, r * 128:(r + 1) * 128] = st[r * 128:(r + 1) * 128, :].T
        delta = delta_ref[dev]
        turned = pltpu.roll(delta, 64, 1)
        first = jnp.where(odd == 0, delta, turned)
        second = jnp.where(odd == 0, turned, delta)
        for r in range(4):
            dl_ref[r:r + 1, :] = jnp.where(lane8 < 64, first[2 * r:2 * r + 1], second[2 * r + 1:2 * r + 2])
        m_ref[...] = jnp.full_like(m_ref, -1e20)
        l_ref[...] = jnp.zeros_like(l_ref)
        dqt[...] = jnp.zeros_like(dqt)

        def collect(kb, n):
            live_ref[n] = inv_ref[kb]
            return n + jnp.where((mask_ref[block, kb] > 0) & (kb < block), 1, 0)
        count = lax.fori_loop(0, 64, collect, jnp.int32(0), unroll=8)
        for e in range(4):
            live_ref[count + e] = inv_ref[block]
        last = count // 4

        def places(t):
            out = []
            for e in range(4):
                k = live_ref[t * 4 + e]
                out.append((k // 2, pl.ds(pl.multiple_of((k % 2) * 64, 64), 64)))
            return out

        def bias_of(t):
            parts = []
            for e in range(4):
                index = t * 4 + e
                reach = jnp.where(index < count, 64, jnp.where(index == count, 0, -64))
                parts.append(jnp.where(ahead <= reach, 0.0, -1e30))
            return jnp.concatenate(parts, axis=0)

        def totals(t, masked):
            k = jnp.concatenate([kv_ref[d, 0, r, :] for d, r in places(t)], axis=0)
            s = jnp.dot(k, qt[...], preferred_element_type=F32)
            bias = bias_of(t) if masked else None
            for r in range(4):
                sh = s[:, r * 128:(r + 1) * 128] * (SCALE * LOG2E)
                if masked:
                    sh = sh + bias
                m_old = m_ref[r:r + 1, :]
                m_new = jnp.maximum(m_old, jnp.max(sh, axis=0, keepdims=True))
                p = jnp.exp2(sh - m_new)
                l_ref[r:r + 1, :] = l_ref[r:r + 1, :] * jnp.exp2(m_old - m_new) + jnp.sum(p, axis=0, keepdims=True)
                m_ref[r:r + 1, :] = m_new

        def totals_step(t, _):
            totals(t, False)
            return 0
        lax.fori_loop(0, last, totals_step, 0)
        totals(last, True)
        m_ref[0:4, :] = m_ref[0:4, :] + jnp.log2(l_ref[0:4, :])

        def grads(t, masked):
            at = places(t)
            k = jnp.concatenate([kv_ref[d, 0, r, :] for d, r in at], axis=0)
            v = jnp.concatenate([kv_ref[d, 1, r, :] for d, r in at], axis=0)
            s = jnp.dot(k, qt[...], preferred_element_type=F32)
            dp = jnp.dot(v, dot_[...], preferred_element_type=F32)
            bias = bias_of(t) if masked else None
            ps, dss = [], []
            for r in range(4):
                cols = slice(r * 128, (r + 1) * 128)
                sh = s[:, cols] * (SCALE * LOG2E) - m_ref[r:r + 1, :]
                if masked:
                    sh = sh + bias
                p = jnp.exp2(sh)
                ds = p * (dp[:, cols] - dl_ref[r:r + 1, :])
                ps.append(p.astype(BF))
                dss.append(ds.astype(BF))
            p = jnp.concatenate(ps, axis=1)
            ds = jnp.concatenate(dss, axis=1)
            dv = jnp.dot(p, dos[...], preferred_element_type=F32)
            dk = jnp.dot(ds, qs[...], preferred_element_type=F32)
            for e, (d, r) in enumerate(at):
                dvs[d, r, :] += dv[e * 64:(e + 1) * 64]
                dks[d, r, :] += dk[e * 64:(e + 1) * 64]
            dqt[...] += jnp.dot(k.T, ds, preferred_element_type=F32)

        def grads_step(t, _):
            grads(t, False)
            return 0
        lax.fori_loop(0, last, grads_step, 0)
        grads(last, True)
        for r in range(4):
            out = (dqt[:, r * 128:(r + 1) * 128].T * SCALE).astype(BF)
            for e in range(2):
                if 2 * r + e < HG:
                    dq_ref[dev, pl.ds(half, 64), (2 * r + e) * HD:(2 * r + e + 1) * HD] = out[e * 64:(e + 1) * 64]
        return 0
    lax.fori_loop(0, 4, query_block, 0)

    def write_out(d, _):
        dkv_ref[d, 0] = (dks[d] * SCALE).astype(BF)
        dkv_ref[d, 1] = dvs[d].astype(BF)
        return 0
    lax.fori_loop(0, 32, write_out, 0)


def attn(order, mask, q2, do2, delta2, kvg):
    smem = pl.BlockSpec(memory_space=pltpu.SMEM)
    vmem = pl.BlockSpec(memory_space=pltpu.VMEM)
    return pl.pallas_call(
        attn_kernel,
        out_shape=(jax.ShapeDtypeStruct((2, 128, GW), BF), jax.ShapeDtypeStruct((32, 2, 128, 128), BF)),
        in_specs=[smem, smem, vmem, vmem, vmem, vmem],
        out_specs=(vmem, vmem),
        scratch_shapes=[
            pltpu.SMEM((64,), jnp.int32), pltpu.SMEM((72,), jnp.int32),
            pltpu.VMEM((32, 128, 128), F32), pltpu.VMEM((32, 128, 128), F32),
            pltpu.VMEM((512, 128), BF), pltpu.VMEM((128, 512), BF),
            pltpu.VMEM((512, 128), BF), pltpu.VMEM((128, 512), BF),
            pltpu.VMEM((8, 128), F32), pltpu.VMEM((8, 128), F32), pltpu.VMEM((8, 128), F32),
            pltpu.VMEM((128, 512), F32),
        ],
        cost_estimate=pl.CostEstimate(flops=20_000_000_000, bytes_accessed=8_000_000, transcendentals=8_000_000),
        name="attention",
    )(order, mask, q2, do2, delta2, kvg)


OUT_LINKS = 64
LW = 448


def finish_kernel(order_ref, owner_ref, dkv, dq, x_ref, gain_ref, vis_ref, pgain_ref, wg, w2, proj,
                  tok_ref, enc_ref, w, pj, ring, stage, ysend, yrecv, hg, ng, x8, nsend, nrecv, half_out, half_in,
                  send, recv, loc):
    p = Place()
    links = Links(send, recv)
    partner = p.dev(c=1 - p.c)
    ypeer = p.dev(h=1 - p.h)
    zs = {1: p.dev(dz=1), -1: p.dev(dz=-1)}
    fan = [p.dev(dx=1), p.dev(dx=-1), p.dev(l=1 - p.l)]
    shift = [0, 3, 1, 2]
    rows = lambda dz, n: pl.ds(pl.multiple_of((((p.z + dz + 8) % 8) * 4 + (p.unit + shift[n]) % 4) * WR, 16), WR)
    held = []
    for level in (1, 0, 2):
        for n in range(4):
            held.append(pltpu.make_async_copy(wg.at[level, n], w.at[rows(level - 1, n)], loc.at[len(held)]))
    for i, dz in enumerate((-2, 2)):
        held.append(pltpu.make_async_copy(w2.at[i], w.at[rows(dz, 0)], loc.at[len(held)]))
    for cp in held:
        cp.start()
    pcopy = pltpu.make_async_copy(proj, pj, loc.at[20])
    pcopy.start()
    greet([partner, ypeer, zs[1], zs[-1]] + fan)

    sent = []
    hop = {}
    chip = lambda dz, e: pl.ds(2 * p.chip(dz, 1 - p.h if e == 0 else p.h), 2)
    nt = (((1,), (1,)), ((), ()))

    def pass_on(step, dr, e):
        dest = dr * (5 - step)
        if (step - 1, dr, e) in hop:
            hop[step - 1, dr, e].wait_recv()
            stage[step - 2, (1 - dr) // 2, e] = (
                dkv[chip(dest, e)].astype(F32) + ring[step - 2, (1 - dr) // 2, e].astype(F32)).astype(BF)
            src = stage.at[step - 2, (1 - dr) // 2, e]
        else:
            src = dkv.at[chip(dest, e)]
        hop[step, dr, e] = cp = links.copy(src, ring.at[step - 1, (1 - dr) // 2, e], zs[dr])
        cp.start()
        sent.append(cp)

    wcopies = {}

    def w_send(step, dr):
        if step == 3:
            src, dst = w2.at[(1 - dr) // 2], w.at[rows(-dr * 2, 0)]
        else:
            base = (((p.z - dr * 3 + 16) % 8) * 4 + p.unit) * WR
            src = dst = w.at[pl.ds(pl.multiple_of(base, 16), 64)] if dr == 1 else w.at[pl.ds(pl.multiple_of(base + 64, 16), 48)]
        wcopies[step, dr] = cp = links.copy(src, dst, zs[dr])
        cp.start()
        sent.append(cp)

    def spread(dz, src=None):
        part = w.at[rows(dz, 0)]
        for n, dev in enumerate(fan):
            wcopies[dz, "fan", n] = cp = links.copy(part if src is None else src, part, dev)
            cp.start()
            sent.append(cp)

    def arrived(dz):
        for n in range(3):
            wcopies[dz, "fan", n].wait_recv()

    def multiply(dz):
        level = (p.z + dz + 8) % 8
        part = w[pl.ds(pl.multiple_of(level * LW, 16), LW), 0:GW]
        ng[level] = lax.dot_general(hg[:, 0:GW], part, nt, preferred_element_type=F32)

    pass_on(1, 1, 0)
    pass_on(1, -1, 1)
    pass_on(2, 1, 1)
    pass_on(2, -1, 0)
    for dr in (1, -1):
        w_send(3, dr)
        spread(-2 * dr, w2.at[(1 - dr) // 2])
    for d in range(2):
        hg[d * 128:(d + 1) * 128, 0:GW] = dq[d]
    ready = iter(range(3))

    def near(dz):
        i = next(ready)
        for cp in held[4 * i:4 * i + 4]:
            cp.wait()
        multiply(dz)

    near(0)
    pass_on(2, 1, 0)
    pass_on(2, -1, 1)
    near(-1)
    for dr in (1, -1):
        wcopies[3, dr].wait_recv()
        w_send(4, dr)
        spread(-3 * dr)
    for dr in (1, -1):
        pass_on(3, dr, 0)
    near(1)
    for dr in (1, -1):
        pass_on(3, dr, 1)
    for cp in held[12:]:
        cp.wait()
    for dr in (1, -1):
        wcopies[4, dr].wait_recv()
    spread(4)
    for dr in (1, -1):
        pass_on(4, dr, 0)
    for dr in (1, -1):
        arrived(-2 * dr)
        multiply(-2 * dr)
    for dr in (1, -1):
        pass_on(4, dr, 1)
    square = jnp.zeros((128, 1), F32)
    for i in range(8):
        xi = x_ref[:, i * LW:(i + 1) * LW]
        x8[i] = xi
        xf = xi.astype(F32)
        square = square + jnp.sum(xf * xf, axis=1, keepdims=True)
    inverse = lax.rsqrt(square * (1.0 / D) + EPSILON)
    for dr in (1, -1):
        hop[4, dr, 0].wait_recv()
    ysend[...] = (dkv[chip(0, 0)].astype(F32) + ring[3, 0, 0].astype(F32) + ring[3, 1, 0].astype(F32)).astype(BF)
    ycopy = links.copy(ysend, yrecv, ypeer)
    ycopy.start()
    sent.append(ycopy)
    for dr in (1, -1):
        arrived(-3 * dr)
        multiply(-3 * dr)
    for dr in (1, -1):
        hop[4, dr, 1].wait_recv()
    arrived(4)
    multiply(4)
    ycopy.wait_recv()
    total = (dkv[chip(0, 1)].astype(F32) + ring[3, 0, 1].astype(F32) + ring[3, 1, 1].astype(F32) + yrecv[...].astype(F32)).astype(BF)
    for d in range(2):
        hg[d * 128:(d + 1) * 128, GW:GW + HD] = total[d, 0]
        hg[d * 128:(d + 1) * 128, GW + HD:CW] = total[d, 1]
    theirs = pl.ds(pl.multiple_of((1 - p.c) * 128, 128), 128)
    ours = pl.ds(pl.multiple_of(p.c * 128, 128), 128)
    swaps = []
    for i in range(8):
        ng[i] += lax.dot_general(hg[:, GW:CW], w[i * LW:(i + 1) * LW, GW:CW], nt, preferred_element_type=F32)
        nsend[i] = ng[i, theirs, :].astype(BF)
        cp = links.copy(nsend.at[i], nrecv.at[i], partner)
        cp.start()
        swaps.append(cp)
        sent.append(cp)
    weighted_sum = jnp.zeros((128, 1), F32)
    for i in range(8):
        swaps[i].wait_recv()
        low = (ng[i, ours, :] + nrecv[i].astype(F32)).astype(BF)
        u = low.astype(F32) * gain_ref[i * LW:(i + 1) * LW].reshape(1, LW)
        ng[i, 0:128, :] = u
        weighted_sum = weighted_sum + jnp.sum(u * x8[i].astype(F32), axis=1, keepdims=True)
    slope = inverse * inverse * inverse * (weighted_sum * (1.0 / D))
    for i in range(8):
        tok_ref[:, i * LW:(i + 1) * LW] = (inverse * ng[i, 0:128, :] - x8[i].astype(F32) * slope).astype(BF)

    first_block = order_ref[2 * p.s]
    second_block = order_ref[2 * p.s + 1]
    frame = jnp.int32(0)
    for f in range(32):
        frame = frame + jnp.where(owner_ref[f] == p.s, f, 0)
    keep_first = first_block // 2 == frame
    kept_block = jnp.where(keep_first, first_block, second_block)
    leading = kept_block % 2 == 0
    half_out[...] = jnp.where(keep_first, tok_ref[64:, :], tok_ref[:64, :])
    hcopy = links.copy(half_out, half_in, partner)
    hcopy.start()
    sent.append(hcopy)
    kept = jnp.where(keep_first, tok_ref[:64, :], tok_ref[64:, :])
    vis = vis_ref[...].astype(F32)
    centered = vis - jnp.mean(vis, axis=1, keepdims=True)
    deviation = lax.rsqrt(jnp.mean(centered * centered, axis=1, keepdims=True) + EPSILON)
    normed = centered * deviation
    pcopy.wait()
    hcopy.wait_recv()
    got = half_in[...]
    framed = jnp.concatenate([jnp.where(leading, kept, got), jnp.where(leading, got, kept)], axis=0)
    post = lax.dot_general(framed, pj[...], nt, preferred_element_type=F32)
    weighted = post * pgain_ref[...].reshape(1, CW)
    enc_ref[...] = (deviation * (
        weighted - jnp.mean(weighted, axis=1, keepdims=True)
        - normed * jnp.mean(weighted * normed, axis=1, keepdims=True))).astype(BF)
    for cp in sent:
        cp.wait_send()


def finish(order, owner, dkv, dq, x, gain, vis, pgain, wg, w2, proj):
    smem = pl.BlockSpec(memory_space=pltpu.SMEM)
    vmem = pl.BlockSpec(memory_space=pltpu.VMEM)
    hbm = pl.BlockSpec(memory_space=pl.ANY)
    block = (2, 2, 128, HD)
    return pl.pallas_call(
        finish_kernel,
        out_shape=(jax.ShapeDtypeStruct((128, D), BF), jax.ShapeDtypeStruct((128, CW), BF)),
        in_specs=[smem, smem] + [vmem] * 6 + [hbm] * 3,
        out_specs=(vmem, vmem),
        scratch_shapes=[
            pltpu.VMEM((D, CW), BF), pltpu.VMEM((CW, D), BF),
            pltpu.VMEM((4, 2, 2) + block, BF), pltpu.VMEM((3, 2, 2) + block, BF),
            pltpu.VMEM(block, BF), pltpu.VMEM(block, BF),
            pltpu.VMEM((256, CW), BF), pltpu.VMEM((8, 256, LW), F32), pltpu.VMEM((8, 128, LW), BF),
            pltpu.VMEM((8, 128, LW), BF), pltpu.VMEM((8, 128, LW), BF),
            pltpu.VMEM((64, D), BF), pltpu.VMEM((64, D), BF),
            pltpu.SemaphoreType.DMA((OUT_LINKS,)), pltpu.SemaphoreType.DMA((OUT_LINKS,)),
            pltpu.SemaphoreType.DMA((21,)),
        ],
        compiler_params=pltpu.CompilerParams(collective_id=1, has_side_effects=True),
        name="finish",
    )(order, owner, dkv, dq, x, gain, vis, pgain, wg, w2, proj)


def body(queries, keys, values, out_grad, row_delta, layer_input, norm_gain, qkv_weight,
         block_order, block_mask, frame_owner, vision_features, post_gain, projector):
    delta = jnp.pad(jnp.transpose(row_delta).reshape(2, HG, 128), ((0, 0), (0, 1), (0, 0)))
    kvg, q2, do2, delta2, wg, w2 = gather(keys, values, queries, out_grad, delta, qkv_weight)
    dq, dkv = attn(block_order, block_mask, q2, do2, delta2, kvg)
    token_grad, encoder_grad = finish(block_order, frame_owner, dkv, dq, layer_input, norm_gain, vision_features[0],
                                      post_gain, wg, w2, projector)
    return token_grad, encoder_grad[None]


def solution(mesh):
    rows = P(("batch", "seq"), None)
    cube = P(("batch", "seq"), None, None)
    placed = (rows, rows, rows, rows, rows, rows, P(), P("seq", None), P("batch"), P("batch", None), P("batch"),
              cube, P(), P())
    return jax.shard_map(body, mesh=mesh, in_specs=placed, out_specs=(rows, cube), check_vma=False)
```

time: 640 us -> 126 us (0.20)
  starting transfers between devices: 229 us -> 0 us
  waiting for transfers between devices: 155 us -> 0 us
  Pallas kernels: 0 us -> 120 us
  matrix products: 94.1 us -> 0 us
  local copies, waits for them, and re-layouts: 90.5 us -> 5.16 us
  loops' own time: 25.2 us -> 0 us
  other arithmetic: 23.4 us -> 0 us
  between operations: 18.9 us -> 0.65 us
    ppermute x127 -> x0, starting transfers between devices: 229 us -> none  [the longest x126 223 us: shifted(): return lax.ppermute(value, axis, pairs)]
    pallas_call x0 -> x3, Pallas kernels: none -> 120 us  [the longest x1 51.4 us: finish(): pl.pallas_call(finish_kernel, out_shape=(jax.ShapeDtypeStruct((128, D), B...]
    dot_general x259 -> x0, matrix products: 94.1 us -> none  [the longest x64 20.6 us: score_block(): jnp.einsum('qkgd,tkd->kgqt', query_part, keys_here, preferred_element_typ...]
    ppermute x127 -> x0, waiting for transfers between devices: 78.3 us -> none  [the longest x126 78.3 us: shifted(): return lax.ppermute(value, axis, pairs)]
    all_gather x2 -> x0, waiting for transfers between devices: 75.2 us -> none  [the longest x1 75.1 us: body(): key_piece = lax.all_gather(keys, 'seq', axis=0, tiled=True)]
    dynamic_slice x64 -> x0, local copies, waits for them, and re-layouts: 48.1 us -> none  [body(): lax.scan(absorb, zero_stats, (stacked, jnp.arange(shards, dtype=jnp.int32)))]
    while x95 -> x0, local copies, waits for them, and re-layouts: 27.5 us -> none
    another operation x2 -> x0, loops' own time: 25.2 us -> none  [the longest x1 22.9 us: body(): lax.scan(absorb, zero_stats, (stacked, jnp.arange(shards, dtype=jnp.int32)))]
  transfers between devices with their start and end apart: 129 -> 0, of which waited for: 64 -> 0; matrix products, arithmetic and copies ran while one was open for 30% -> 0% of each run, Pallas kernels for 0% -> 0%
where the time goes in v1:
time: 126 us
  Pallas kernels  120 us (95%)
  local copies, waits for them, and re-layouts  5.16 us (4%)
    pallas_call x1, Pallas kernels, finish(): pl.pallas_call(finish_kernel, out_shape=(jax.ShapeDtypeStruct((128, D), B...  51.4 us
    pallas_call x1, Pallas kernels, gather(): pl.pallas_call(gather_kernel, out_shape=(jax.ShapeDtypeStruct((32, 2, 128...  49.4 us
    pallas_call x1, Pallas kernels, attn(): pl.pallas_call(attn_kernel, out_shape=(jax.ShapeDtypeStruct((2, 128, GW),...  19.1 us
    unnamed x2, local copies, waits for them, and re-layouts  3.86 us

profile of v1, /device:TPU:1, one launch (start us, length us, event | category | flops | bytes accessed | tf_op | source)
XLA Modules:
  0.0 125.7 jit_solution(5866843618524421649)
XLA Ops:
  0.6 0.7 reshape.7
  1.3 0.6 pad.4.dl_ref
  1.9 49.4 %gather.1 = (bf16[32,2,128,128]{3,2,1,0:T(8,128)(2,1)}, bf16[2,128,896]{2,1,0:T(8,128)(2,1)}, bf16[2,128,896]{2,1,0:T(8,128)(2,1)}, f32[2,8,128]{2,1,0:T(8,128)}...) custom-call(bf16[128,256]{1,0:T(8,128)(2,1)} %k_ref.1, bf16[128,256]{1,0:T(8,128)(2,1)} %v_ref.1, ...), custom_call_target="tpu_custom_call" | custom-call | tf_op jit(solution)/shard_map/gather/pallas_call | solution.py:250
  51.3 19.1 %attention.1 = (bf16[2,128,896]{2,1,0:T(8,128)(2,1)}, bf16[32,2,128,128]{3,2,1,0:T(8,128)(2,1)}) custom-call(s32[64]{0:T(128)} %order_ref.3, s32[64,64]{1,0:T(8,128)} %mask_ref.1, bf16[2,128,896]{2,1,0:T(8,128)(2,1)} %get-tuple-element.12.q_ref, bf16[2,128,896]{2,1,0:T(8,128)(2,1)} %get-tuple-element.13.do_ref, f32[2,8,128]{2,1,0:T(8,128)} %get-tuple-element.14.delta_ref, ...), custom_call_target="tpu_custom_call" | custom-call | flops 20000000000 | bytes 8000000 | tf_op jit(solution)/shard_map/attention/pallas_call | solution.py:392
  70.4 51.4 %finish.1 = (bf16[128,3584]{1,0:T(8,128)(2,1)}, bf16[128,1152]{1,0:T(8,128)(2,1)}) custom-call(s32[64]{0:T(128)} %order_ref.3, s32[32]{0:T(128)} %owner_ref.1, bf16[32,2,128,128]{3,2,1,0:T(8,128)(2,1)} %get-tuple-element.16.dkv, bf16[2,128,896]{2,1,0:T(8,128)(2,1)} %get-tuple-element.17.dq, bf16[128,3584]{1,0:T(8,128)(2,1)} %x_ref.1, f32[3584]{0:T(1024)} %gain_ref.1, ...), custom_call_target="tpu_custom_call" | custom-call | tf_op jit(solution)/shard_map/finish/pallas_call | solution.py:606
  121.8 2.2 %copy.18 = bf16[128,3584]{1,0:T(8,128)(2,1)} copy(bf16[128,3584]{1,0:T(8,128)(2,1)} %get-tuple-element.24) | data formatting | bytes 1835008
  124.0 1.7 %copy.19 = bf16[1,128,1152]{2,1,0:T(8,128)(2,1)} copy(bf16[1,128,1152]{2,1,0:T(8,128)(2,1)} %bitcast.3) | data formatting | bytes 589824

commit v2 on v1

--- a/solution.py
+++ b/solution.py
@@ -215,8 +215,8 @@
         for cp in to_across:
             cp.start()
     kv_step(1, 1)
+    w_take(1)
     kv_step(2, 0)
-    w_take(1)
     kv_step(2, 1)
     kv_step(3, 0)
     w_take(2)
@@ -296,17 +296,20 @@
         l_ref[...] = jnp.zeros_like(l_ref)
         dqt[...] = jnp.zeros_like(dqt)
 
-        def collect(kb, n):
-            live_ref[n] = inv_ref[kb]
-            return n + jnp.where((mask_ref[block, kb] > 0) & (kb < block), 1, 0)
-        count = lax.fori_loop(0, 64, collect, jnp.int32(0), unroll=8)
+        def collect(g, n):
+            for e in range(8):
+                kb = g * 8 + e
+                live_ref[n] = inv_ref[kb]
+                n = n + jnp.where((mask_ref[block, kb] > 0) & (kb < block), 1, 0)
+            return n
+        count = lax.fori_loop(0, (block + 7) // 8, collect, jnp.int32(0))
         for e in range(4):
             live_ref[count + e] = inv_ref[block]
         last = count // 4
 
-        def places(t):
+        def places(t, n=4):
             out = []
-            for e in range(4):
+            for e in range(n):
                 k = live_ref[t * 4 + e]
                 out.append((k // 2, pl.ds(pl.multiple_of((k % 2) * 64, 64), 64)))
             return out
@@ -319,8 +322,8 @@
                 parts.append(jnp.where(ahead <= reach, 0.0, -1e30))
             return jnp.concatenate(parts, axis=0)
 
-        def totals(t, masked):
-            k = jnp.concatenate([kv_ref[d, 0, r, :] for d, r in places(t)], axis=0)
+        def totals(t, masked, n=4):
+            k = jnp.concatenate([kv_ref[d, 0, r, :] for d, r in places(t, n)], axis=0)
             s = jnp.dot(k, qt[...], preferred_element_type=F32)
             bias = bias_of(t) if masked else None
             for r in range(4):
@@ -334,14 +337,18 @@
                 m_ref[r:r + 1, :] = m_new
 
         def totals_step(t, _):
-            totals(t, False)
+            totals(2 * t, False, 8)
             return 0
-        lax.fori_loop(0, last, totals_step, 0)
+        lax.fori_loop(0, last // 2, totals_step, 0)
+
+        @pl.when(last % 2 == 1)
+        def _():
+            totals(last - 1, False)
         totals(last, True)
         m_ref[0:4, :] = m_ref[0:4, :] + jnp.log2(l_ref[0:4, :])
 
-        def grads(t, masked):
-            at = places(t)
+        def grads(t, masked, n=4):
+            at = places(t, n)
             k = jnp.concatenate([kv_ref[d, 0, r, :] for d, r in at], axis=0)
             v = jnp.concatenate([kv_ref[d, 1, r, :] for d, r in at], axis=0)
             s = jnp.dot(k, qt[...], preferred_element_type=F32)
@@ -367,9 +374,13 @@
             dqt[...] += jnp.dot(k.T, ds, preferred_element_type=F32)
 
         def grads_step(t, _):
-            grads(t, False)
+            grads(2 * t, False, 8)
             return 0
-        lax.fori_loop(0, last, grads_step, 0)
+        lax.fori_loop(0, last // 2, grads_step, 0)
+
+        @pl.when(last % 2 == 1)
+        def _():
+            grads(last - 1, False)
         grads(last, True)
         for r in range(4):
             out = (dqt[:, r * 128:(r + 1) * 128].T * SCALE).astype(BF)
@@ -419,7 +430,7 @@
     partner = p.dev(c=1 - p.c)
     ypeer = p.dev(h=1 - p.h)
     zs = {1: p.dev(dz=1), -1: p.dev(dz=-1)}
-    fan = [p.dev(dx=1), p.dev(dx=-1), p.dev(l=1 - p.l)]
+    fan = [p.dev(dx=1), p.dev(dx=-1), p.dev(l=1 - p.l), p.dev(h=1 - p.h, l=1 - p.l)]
     shift = [0, 3, 1, 2]
     rows = lambda dz, n: pl.ds(pl.multiple_of((((p.z + dz + 8) % 8) * 4 + (p.unit + shift[n]) % 4) * WR, 16), WR)
     held = []
@@ -465,14 +476,16 @@
         sent.append(cp)
 
     def spread(dz, src=None):
-        part = w.at[rows(dz, 0)]
+        level = ((p.z + dz + 8) % 8) * 4 + p.unit
         for n, dev in enumerate(fan):
-            wcopies[dz, "fan", n] = cp = links.copy(part if src is None else src, part, dev)
+            first, count = ((0, WR), (0, WR), (0, 64), (64, 48))[n]
+            part = w.at[pl.ds(pl.multiple_of(level * WR + first, 16), count)]
+            wcopies[dz, "fan", n] = cp = links.copy(part if src is None else src.at[pl.ds(first, count)], part, dev)
             cp.start()
             sent.append(cp)
 
     def arrived(dz):
-        for n in range(3):
+        for n in range(4):
             wcopies[dz, "fan", n].wait_recv()
 
     def multiply(dz):

time: 126 us -> 124 us (0.984); the launches traced: 126 us -> 125 us
  no operation moved by 1% of the time
where the time goes in v2:
time: 124 us; the launch traced here: 125 us
  Pallas kernels  119 us (96%)
  local copies, waits for them, and re-layouts  5.16 us (4%)
    pallas_call x1, Pallas kernels, finish(): pl.pallas_call(finish_kernel, out_shape=(jax.ShapeDtypeStruct((128, D), B...  51.5 us
    pallas_call x1, Pallas kernels, gather(): pl.pallas_call(gather_kernel, out_shape=(jax.ShapeDtypeStruct((32, 2, 128...  49.4 us
    pallas_call x1, Pallas kernels, attn(): pl.pallas_call(attn_kernel, out_shape=(jax.ShapeDtypeStruct((2, 128, GW),...  18.7 us
    unnamed x2, local copies, waits for them, and re-layouts  3.86 us

profile of v2, /device:TPU:1, one launch (start us, length us, event | category | flops | bytes accessed | tf_op | source)
XLA Modules:
  0.0 125.3 jit_solution(4690867412567047538)
XLA Ops:
  0.6 0.7 reshape.7
  1.3 0.6 pad.4.dl_ref
  1.9 49.4 %gather.1 = (bf16[32,2,128,128]{3,2,1,0:T(8,128)(2,1)}, bf16[2,128,896]{2,1,0:T(8,128)(2,1)}, bf16[2,128,896]{2,1,0:T(8,128)(2,1)}, f32[2,8,128]{2,1,0:T(8,128)}...) custom-call(bf16[128,256]{1,0:T(8,128)(2,1)} %k_ref.1, bf16[128,256]{1,0:T(8,128)(2,1)} %v_ref.1, ...), custom_call_target="tpu_custom_call" | custom-call | tf_op jit(solution)/shard_map/gather/pallas_call | solution.py:250
  51.3 18.7 %attention.1 = (bf16[2,128,896]{2,1,0:T(8,128)(2,1)}, bf16[32,2,128,128]{3,2,1,0:T(8,128)(2,1)}) custom-call(s32[64]{0:T(128)} %order_ref.3, s32[64,64]{1,0:T(8,128)} %mask_ref.1, bf16[2,128,896]{2,1,0:T(8,128)(2,1)} %get-tuple-element.12.q_ref, bf16[2,128,896]{2,1,0:T(8,128)(2,1)} %get-tuple-element.13.do_ref, f32[2,8,128]{2,1,0:T(8,128)} %get-tuple-element.14.delta_ref, ...), custom_call_target="tpu_custom_call" | custom-call | flops 20000000000 | bytes 8000000 | tf_op jit(solution)/shard_map/attention/pallas_call | solution.py:403
  70.0 51.5 %finish.1 = (bf16[128,3584]{1,0:T(8,128)(2,1)}, bf16[128,1152]{1,0:T(8,128)(2,1)}) custom-call(s32[64]{0:T(128)} %order_ref.3, s32[32]{0:T(128)} %owner_ref.1, bf16[32,2,128,128]{3,2,1,0:T(8,128)(2,1)} %get-tuple-element.16.dkv, bf16[2,128,896]{2,1,0:T(8,128)(2,1)} %get-tuple-element.17.dq, bf16[128,3584]{1,0:T(8,128)(2,1)} %x_ref.1, f32[3584]{0:T(1024)} %gain_ref.1, ...), custom_call_target="tpu_custom_call" | custom-call | tf_op jit(solution)/shard_map/finish/pallas_call | solution.py:619
  121.4 2.2 %copy.18 = bf16[128,3584]{1,0:T(8,128)(2,1)} copy(bf16[128,3584]{1,0:T(8,128)(2,1)} %get-tuple-element.24) | data formatting | bytes 1835008
  123.6 1.7 %copy.19 = bf16[1,128,1152]{2,1,0:T(8,128)(2,1)} copy(bf16[1,128,1152]{2,1,0:T(8,128)(2,1)} %bitcast.3) | data formatting | bytes 589824

commit v3 on v2

--- a/solution.py
+++ b/solution.py
@@ -442,7 +442,6 @@
     for cp in held:
         cp.start()
     pcopy = pltpu.make_async_copy(proj, pj, loc.at[20])
-    pcopy.start()
     greet([partner, ypeer, zs[1], zs[-1]] + fan)
 
     sent = []
@@ -511,6 +510,7 @@
         multiply(dz)
 
     near(0)
+    pcopy.start()
     pass_on(2, 1, 0)
     pass_on(2, -1, 1)
     near(-1)

time: 124 us -> 124 us (level)
  no operation moved by 1% of the time
where the time goes in v3:
time: 124 us; the launch traced here: 125 us
  Pallas kernels  119 us (96%)
  local copies, waits for them, and re-layouts  5.16 us (4%)
    pallas_call x1, Pallas kernels, finish(): pl.pallas_call(finish_kernel, out_shape=(jax.ShapeDtypeStruct((128, D), B...  50.8 us
    pallas_call x1, Pallas kernels, gather(): pl.pallas_call(gather_kernel, out_shape=(jax.ShapeDtypeStruct((32, 2, 128...  49.4 us
    pallas_call x1, Pallas kernels, attn(): pl.pallas_call(attn_kernel, out_shape=(jax.ShapeDtypeStruct((2, 128, GW),...  19.2 us
    unnamed x2, local copies, waits for them, and re-layouts  3.86 us

profile of v3, /device:TPU:1, one launch (start us, length us, event | category | flops | bytes accessed | tf_op | source)
XLA Modules:
  0.0 125.1 jit_solution(14055761430511984976)
XLA Ops:
  0.6 0.7 reshape.7
  1.3 0.6 pad.4.dl_ref
  1.9 49.4 %gather.1 = (bf16[32,2,128,128]{3,2,1,0:T(8,128)(2,1)}, bf16[2,128,896]{2,1,0:T(8,128)(2,1)}, bf16[2,128,896]{2,1,0:T(8,128)(2,1)}, f32[2,8,128]{2,1,0:T(8,128)}...) custom-call(bf16[128,256]{1,0:T(8,128)(2,1)} %k_ref.1, bf16[128,256]{1,0:T(8,128)(2,1)} %v_ref.1, ...), custom_call_target="tpu_custom_call" | custom-call | tf_op jit(solution)/shard_map/gather/pallas_call | solution.py:250
  51.3 19.2 %attention.1 = (bf16[2,128,896]{2,1,0:T(8,128)(2,1)}, bf16[32,2,128,128]{3,2,1,0:T(8,128)(2,1)}) custom-call(s32[64]{0:T(128)} %order_ref.3, s32[64,64]{1,0:T(8,128)} %mask_ref.1, bf16[2,128,896]{2,1,0:T(8,128)(2,1)} %get-tuple-element.12.q_ref, bf16[2,128,896]{2,1,0:T(8,128)(2,1)} %get-tuple-element.13.do_ref, f32[2,8,128]{2,1,0:T(8,128)} %get-tuple-element.14.delta_ref, ...), custom_call_target="tpu_custom_call" | custom-call | flops 20000000000 | bytes 8000000 | tf_op jit(solution)/shard_map/attention/pallas_call | solution.py:403
  70.5 50.8 %finish.1 = (bf16[128,3584]{1,0:T(8,128)(2,1)}, bf16[128,1152]{1,0:T(8,128)(2,1)}) custom-call(s32[64]{0:T(128)} %order_ref.3, s32[32]{0:T(128)} %owner_ref.1, bf16[32,2,128,128]{3,2,1,0:T(8,128)(2,1)} %get-tuple-element.16.dkv, bf16[2,128,896]{2,1,0:T(8,128)(2,1)} %get-tuple-element.17.dq, bf16[128,3584]{1,0:T(8,128)(2,1)} %x_ref.1, f32[3584]{0:T(1024)} %gain_ref.1, ...), custom_call_target="tpu_custom_call" | custom-call | tf_op jit(solution)/shard_map/finish/pallas_call | solution.py:619
  121.3 2.2 %copy.18 = bf16[128,3584]{1,0:T(8,128)(2,1)} copy(bf16[128,3584]{1,0:T(8,128)(2,1)} %get-tuple-element.24) | data formatting | bytes 1835008
  123.4 1.7 %copy.19 = bf16[1,128,1152]{2,1,0:T(8,128)(2,1)} copy(bf16[1,128,1152]{2,1,0:T(8,128)(2,1)} %bitcast.3) | data formatting | bytes 589824
